TPU v7x, 32 devices: a whole 2x2x4 slice. The times are simulated.
32 devices in a mesh: group: 4 (over x, core), seq: 2 (over y), expert: 4 (over z).
Axes of the slice: x: 2, y: 2, z: 4, core: 2. Of those that a mesh axis runs over, the one named last changes fastest.
Arguments:
- queries: bfloat16 [16, 32, 128], P('expert', 'group')
- keys: bfloat16 [16, 256, 8, 128], P('expert', 'seq', 'group')
- values: bfloat16 [16, 256, 8, 128], P('expert', 'seq', 'group'), may hold values from -48 to 48
- block_of_slot: int32 [16, 16], P('expert', 'seq'), may hold values from 0 to 15, each once within a row
- lengths: int32 [16], P('expert'), may hold values from 128 to 256
- out_proj: bfloat16 [4096, 4096], P('group', 'seq'), may hold values from -0.09375 to 0.09375
- residual: bfloat16 [16, 4096], P('expert', 'seq'), may hold values from -6 to 6
- norm_gain: bfloat16 [4096], replicated, may hold values from 0.25 to 1.75
- router: bfloat16 [4096, 8], replicated, may hold values from -0.09375 to 0.09375
- routes: int32 [16, 2], P('expert'), may hold values from 0 to 7, all different within a row; in each aligned block of 4 rows (0 to 3, 4 to 7, ...) at most 2 rows name the same one
- w_gate: bfloat16 [8, 4096, 14336], P('expert', None, ('group', 'seq')), may hold values from -0.09375 to 0.09375
- w_up: bfloat16 [8, 4096, 14336], P('expert', None, ('group', 'seq')), may hold values from -0.09375 to 0.09375
- w_down: bfloat16 [8, 14336, 4096], P('expert', ('group', 'seq')), may hold values from -0.046875 to 0.046875
Outputs:
- layer_out: bfloat16 [16, 4096], P('expert', 'seq')
Inputs may be any that keep to these rules, and one draw needn't show every extreme that they name: `block_of_slot`: each row lists every logical block once. `routes`: the two ids of a row differ; among the 4 rows of one device no expert is named more than 2 times, and in some such blocks one expert is named exactly 2 times.
All inputs are finite; a program needn't handle non-finite values.
Results may differ from a plain program's by a relative error of at most 0.013.
Values may be sent and summed in bfloat16 or wider, within the bound.
No kernel may reach another device: no remote copies, remote signals or barrier semaphores. Data moves between devices by JAX's collectives and lax.ppermute only.
A program may use at most 128 MiB of HBM per device.

v0:
```python
import jax
import jax.numpy as jnp
from jax import lax
from jax.sharding import PartitionSpec as P

BLOCK = 16
CAPACITY = 2
masked_score = -1e30


def combined_all(value, axis, combine):
    everything = jax.tree.map(lambda part: lax.all_gather(part, axis), value)
    initial = jax.tree.map(lambda part: part[0], everything)

    def hop(k, so_far):
        return combine(so_far, jax.tree.map(lambda part: part[k], everything))

    return lax.fori_loop(1, lax.axis_size(axis), hop, initial)


def combine_carry(earlier, later):
    high_a, total_a, sums_a = earlier
    high_b, total_b, sums_b = later
    highest = jnp.maximum(high_a, high_b)
    scale_a = jnp.exp(high_a - highest)
    scale_b = jnp.exp(high_b - highest)
    return (
        highest,
        total_a * scale_a + total_b * scale_b,
        sums_a * scale_a[..., None] + sums_b * scale_b[..., None],
    )


def shards(
    queries,
    keys,
    values,
    block_of_slot,
    lengths,
    out_proj,
    residual,
    norm_gain,
    router,
    routes,
    w_gate,
    w_up,
    w_down,
):
    batch_rows, local_heads, head_dim = queries.shape
    span_len = keys.shape[1]
    kv_local = keys.shape[2]
    per_kv = local_heads // kv_local
    grouped = queries.reshape(batch_rows, kv_local, per_kv, head_dim)
    scores = jnp.einsum(
        "rkgd,rlkd->rkgl", grouped, keys, preferred_element_type=jnp.float32
    ) * head_dim ** (-0.5)
    offsets = jnp.arange(BLOCK, dtype=jnp.int32)
    position = (block_of_slot[:, :, None] * BLOCK + offsets[None, None, :]).reshape(
        batch_rows, span_len
    )
    visible = (position < lengths[:, None])[:, None, None, :]
    masked = jnp.where(visible, scores, masked_score)
    highest = jnp.max(masked, axis=-1)
    probs = jnp.where(visible, jnp.exp(masked - highest[..., None]), 0.0)
    totals = jnp.sum(probs, axis=-1)
    weighted = jnp.einsum(
        "rkgl,rlkd->rkgd", probs.astype(jnp.bfloat16), values, preferred_element_type=jnp.float32
    )
    local_carry = (highest, totals, weighted)
    highest, totals, weighted = combined_all(local_carry, "seq", combine_carry)
    attended = (
        (weighted / totals[..., None])
        .astype(jnp.bfloat16)
        .reshape(batch_rows, local_heads * head_dim)
    )
    partial_value = jnp.dot(attended, out_proj, preferred_element_type=jnp.float32)
    attention = lax.psum(partial_value, "group")
    hidden = residual.astype(jnp.float32) + attention
    full_rows = lax.all_gather(hidden, "seq", axis=1, tiled=True)
    meansq = jnp.mean(full_rows * full_rows, axis=-1, keepdims=True)
    normed = (full_rows * lax.rsqrt(meansq + 1e-05) * norm_gain.astype(jnp.float32)).astype(
        jnp.bfloat16
    )
    logits = jnp.dot(normed, router, preferred_element_type=jnp.float32)
    experts = router.shape[1]
    onehot = (routes[:, :, None] == jnp.arange(experts, dtype=jnp.int32)[None, None, :]).astype(
        jnp.int32
    )
    chosen = jnp.sum(onehot.astype(jnp.float32) * logits[:, None, :], axis=-1)
    gate_probs = jax.nn.softmax(chosen, axis=-1)
    per_row = jnp.sum(onehot, axis=1)
    earlier = jnp.cumsum(per_row, axis=0) - per_row
    slot_index = jnp.sum(onehot * earlier[:, None, :], axis=2)
    in_slot = (
        slot_index[:, :, None] == jnp.arange(CAPACITY, dtype=jnp.int32)[None, None, :]
    ).astype(jnp.int32)
    chart = onehot[:, :, :, None] * in_slot[:, :, None, :]
    picker = jnp.sum(chart, axis=1).astype(jnp.bfloat16)
    outbound = jnp.einsum("rec,rd->ecd", picker, normed, preferred_element_type=jnp.float32).astype(
        jnp.bfloat16
    )
    expert_devs = lax.axis_size("expert")
    local_experts = experts // expert_devs
    model_width = normed.shape[1]
    outbound = outbound.reshape(expert_devs, local_experts, CAPACITY, model_width)
    inbound = lax.all_to_all(outbound, "expert", split_axis=0, concat_axis=0, tiled=True)
    gate_act = jnp.einsum("secd,edf->secf", inbound, w_gate, preferred_element_type=jnp.float32)
    upper = jnp.einsum("secd,edf->secf", inbound, w_up, preferred_element_type=jnp.float32)
    activated = (jax.nn.silu(gate_act) * upper).astype(jnp.bfloat16)
    down_terms = jnp.einsum("secf,efd->secd", activated, w_down, preferred_element_type=jnp.float32)
    summed = lax.psum(down_terms.astype(jnp.bfloat16), ("group", "seq")).astype(jnp.float32)
    col_width = summed.shape[3] // lax.axis_size("seq")
    my_cols = lax.dynamic_slice_in_dim(summed, lax.axis_index("seq") * col_width, col_width, 3)
    returned = lax.all_to_all(
        my_cols.astype(jnp.bfloat16), "expert", split_axis=0, concat_axis=0, tiled=True
    )
    returned = returned.reshape(experts, CAPACITY, returned.shape[3]).astype(jnp.float32)
    mixing = jnp.sum(gate_probs[:, :, None, None] * chart.astype(jnp.float32), axis=1)
    expert_mix = jnp.einsum("rec,ecd->rd", mixing, returned, precision=lax.Precision.HIGHEST)
    return (hidden + expert_mix).astype(jnp.bfloat16)


def solution(mesh):
    return jax.shard_map(
        shards,
        mesh=mesh,
        in_specs=(
            P("expert", "group", None),
            P("expert", "seq", "group", None),
            P("expert", "seq", "group", None),
            P("expert", "seq"),
            P("expert"),
            P("group", "seq"),
            P("expert", "seq"),
            P(),
            P(),
            P("expert", None),
            P("expert", None, ("group", "seq")),
            P("expert", None, ("group", "seq")),
            P("expert", ("group", "seq"), None),
        ),
        out_specs=P("expert", "seq"),
        check_vma=False,
    )
```

profile of v0, /device:TPU:0, one launch (start us, length us, event | category | flops | bytes accessed | tf_op | source)
XLA Modules:
  0.0 164.8 jit_solution(3506737250032493510)
XLA Ops:
  6.5 0.8 fusion.56
  7.3 0.7 fusion.55
  9.0 0.7 add_compare_fusion
  9.8 1.0 fusion.64
  10.8 5.3 %all-gather.1 = f32[8,2,4]{2,1,0:T(2,128)S(1)} all-gather(f32[4,2,4]{2,1,0:T(2,128)S(1)} %get-tuple-element.22), channel_id=3, replica_groups=mesh['group'=4,'seq'=2,'expert'=4] {'seq'}, dimensions={0}, use_global_device_ids=true | all-gather | bytes 384 | tf_op jit(solution)/shard_map/all_gather | solution.py:12
  16.3 1.2 fusion.29
  17.4 4.4 %all-gather = f32[8,2,4,128]{3,2,1,0:T(4,128)S(1)} all-gather(f32[4,2,4,128]{3,2,1,0:T(4,128)S(1)} %fusion.29), channel_id=2, replica_groups=mesh['group'=4,'seq'=2,'expert'=4] {'seq'}, dimensions={0}, use_global_device_ids=true | all-gather | bytes 49152 | tf_op jit(solution)/shard_map/all_gather | solution.py:12
  21.8 4.3 %all-gather.2 = f32[8,2,4]{2,1,0:T(2,128)S(1)} all-gather(f32[4,2,4]{2,1,0:T(2,128)S(1)} %fusion.44), channel_id=4, replica_groups=mesh['group'=4,'seq'=2,'expert'=4] {'seq'}, dimensions={0}, use_global_device_ids=true | all-gather | bytes 384 | tf_op jit(solution)/shard_map/all_gather | solution.py:12
  26.3 2.8 %fusion.65 = f32[4,2048]{1,0:T(4,128)S(1)} fusion(bf16[4,1024]{1,0:T(4,128)(2,1)S(1)} %reshape.183, bf16[1024,2048]{1,0:T(8,128)(2,1)} %param.18), kind=kOutput, calls=%fused_computation.72 | convolution fusion | flops 16777216 | bytes 4235264 | tf_op jit(solution)/shard_map/dot_general | solution.py:76
  29.2 10.3 %psum.14 = f32[4,2048]{1,0:T(4,128)S(1)} all-reduce(f32[4,2048]{1,0:T(4,128)S(1)} %fusion.65), channel_id=1, replica_groups=mesh['group'=4,'seq'=2,'expert'=4] {'group'}, use_global_device_ids=true, to_apply=%region_2.3 | all-reduce | flops 8192 | bytes 65536 | tf_op jit(solution)/shard_map/psum | solution.py:77
  39.5 0.9 select_reduce_fusion
  41.1 4.6 %all_gather.27 = f32[4,4096]{1,0:T(4,128)S(1)} all-gather(f32[4,2048]{1,0:T(4,128)S(1)} %convert_add_fusion), channel_id=1, replica_groups=mesh['group'=4,'seq'=2,'expert'=4] {'seq'}, dimensions={1}, use_global_device_ids=true | all-gather | bytes 98304 | tf_op jit(solution)/shard_map/all_gather | solution.py:79
  47.0 0.8 copy.42
  47.7 5.4 %all-to-all-start = ((bf16[4,2,2,4096]{3,2,1,0:T(2,128)(2,1)}), bf16[4,2,2,4096]{3,2,1,0:T(2,128)(2,1)S(1)}, u32[]{:S(2)}, u32[]{:S(2)}) async-start(bf16[4,2,2,4096]{3,2,1,0:T(2,128)(2,1)} %bitcast.2), calls=%async_computation | async-start | bytes 262144 | tf_op jit(solution)/shard_map/all_to_all | solution.py:106
  53.1 1.0 fusion.66
  54.1 0.9 multiply_reduce_fusion.2
  55.0 4.0 %all-to-all-done = bf16[4,2,2,4096]{3,2,1,0:T(2,128)(2,1)S(1)} async-done(((bf16[4,2,2,4096]{3,2,1,0:T(2,128)(2,1)}), bf16[4,2,2,4096]{3,2,1,0:T(2,128)(2,1)S(1)}, u32[]{:S(2)}, u32[]{:S(2)}) %all-to-all-start) | async-done | bytes 131104 | tf_op jit(solution)/shard_map/all_to_all | solution.py:106
  59.1 11.6 %fusion.12 = f32[4,2,2,1792]{3,0,2,1:T(4,128)S(1)} fusion(bf16[2,4096,1792]{2,1,0:T(8,128)(2,1)} %param.23, bf16[4,2,2,4096]{3,2,1,0:T(2,128)(2,1)S(1)} %all-to-all-done), kind=kOutput, calls=%fused_computation.9 | convolution fusion | flops 234881024 | bytes 29605888 | tf_op jit(solution)/shard_map/secd,edf->secf/dot_general | solution.py:107
  70.6 21.8 %fusion.9 = bf16[4,2,2,4096]{3,0,2,1:T(4,128)(2,1)} fusion(bf16[2,1792,4096]{2,1,0:T(8,128)(2,1)} %param.25, bf16[2,4096,1792]{2,1,0:T(8,128)(2,1)} %param.24, f32[4,2,2,1792]{3,0,2,1:T(4,128)S(1)} %fusion.12, bf16[4,2,2,4096]{3,2,1,0:T(2,128)(2,1)S(1)} %all-to-all-done), kind=kOutput, calls=%fused_computation.8 | convolution fusion | flops 469999616 | bytes 59097088 | tf_op jit(solution)/shard_map/secf,efd->secd/dot_general | solution.py:110
  92.5 52.7 %all-reduce.2.cloned.1.call-done = bf16[4,2,2,4096]{3,0,2,1:T(4,128)(2,1)} async-done(((bf16[4,2,2,4096]{3,0,2,1:T(4,128)(2,1)}), bf16[4,2,2,4096]{3,0,2,1:T(4,128)(2,1)}) %all-reduce.2.cloned.1.call-update) | async-done | bytes 131088 | tf_op jit(solution)/shard_map/psum | solution.py:111
  145.2 0.9 convert_convert_fusion
  146.8 4.6 %all-to-all-start.1 = ((bf16[4,2,2,2048]{3,2,1,0:T(2,128)(2,1)}), bf16[4,2,2,2048]{3,2,1,0:T(2,128)(2,1)S(1)}, u32[]{:S(2)}, u32[]{:S(2)}) async-start(bf16[4,2,2,2048]{3,2,1,0:T(2,128)(2,1)} %copy.37), calls=%async_computation.1 | async-start | bytes 131072 | tf_op jit(solution)/shard_map/all_to_all | solution.py:114
  151.5 5.7 %all-to-all-done.1 = bf16[4,2,2,2048]{3,2,1,0:T(2,128)(2,1)S(1)} async-done(((bf16[4,2,2,2048]{3,2,1,0:T(2,128)(2,1)}), bf16[4,2,2,2048]{3,2,1,0:T(2,128)(2,1)S(1)}, u32[]{:S(2)}, u32[]{:S(2)}) %all-to-all-start.1) | async-done | bytes 65568 | tf_op jit(solution)/shard_map/all_to_all | solution.py:114
  157.1 0.8 fusion.27
  (28 shorter events, 4.1 us)
Async XLA Ops:
  6.5 3.2 %copy-start = (bf16[4,128,2,128]{3,2,1,0:T(2,128)(2,1)S(1)}, bf16[4,128,2,128]{3,2,1,0:T(2,128)(2,1)}, u32[]{:S(2)}) copy-start(bf16[4,128,2,128]{3,2,1,0:T(2,128)(2,1)} %param.14) | copy-start | bytes 786436
  47.7 11.3 %all-to-all-start = ((bf16[4,2,2,4096]{3,2,1,0:T(2,128)(2,1)}), bf16[4,2,2,4096]{3,2,1,0:T(2,128)(2,1)S(1)}, u32[]{:S(2)}, u32[]{:S(2)}) async-start(bf16[4,2,2,4096]{3,2,1,0:T(2,128)(2,1)} %bitcast.2), calls=%async_computation | async-start | bytes 262144 | tf_op jit(solution)/shard_map/all_to_all | solution.py:106
  53.1 92.1 %all-reduce.2.cloned.1.call-start = ((), (), s32[]{:S(2)}) async-start(), calls=%async_computation.2 | async-start | bytes 262144 | tf_op jit(solution)/shard_map/psum | solution.py:111
  146.8 10.3 %all-to-all-start.1 = ((bf16[4,2,2,2048]{3,2,1,0:T(2,128)(2,1)}), bf16[4,2,2,2048]{3,2,1,0:T(2,128)(2,1)S(1)}, u32[]{:S(2)}, u32[]{:S(2)}) async-start(bf16[4,2,2,2048]{3,2,1,0:T(2,128)(2,1)} %copy.37), calls=%async_computation.1 | async-start | bytes 131072 | tf_op jit(solution)/shard_map/all_to_all | solution.py:114
Sparse Core Ops, SparseCore 0:
  92.6 52.6 all-reduce.1
where the time goes:
time: 166 us; the launch traced here: 165 us
  waiting for transfers between devices  62.5 us (38%)
  matrix products  40.5 us (24%)
  blocking collectives  28.9 us (17%)
  between operations  13.5 us (8%)
  starting transfers between devices  9.99 us (6%)
  other arithmetic  7.8 us (5%)
  local copies, waits for them, and re-layouts  1.72 us (1%)
    psum x1, waiting for transfers between devices, shards(): lax.psum(down_terms.astype(jnp.bfloat16), ('group', 'seq'))  52.7 us
    dot_general x1, matrix products, shards(): jnp.einsum('secf,efd->secd', activated, w_down, preferred_element_type=jn...  21.8 us
    all_gather x3, blocking collectives, combined_all(): everything = jax.tree.map(lambda part: lax.all_gather(part, axis), value)  14.1 us
    dot_general x1, matrix products, shards(): jnp.einsum('secd,edf->secf', inbound, w_gate, preferred_element_type=jnp....  11.6 us
    psum x1, blocking collectives, shards(): attention = lax.psum(partial_value, 'group')  10.3 us
    all_to_all x1, waiting for transfers between devices, shards(): lax.all_to_all(my_cols.astype(jnp.bfloat16), 'expert', split_axis=0, conc...  5.66 us
    all_to_all x1, starting transfers between devices, shards(): lax.all_to_all(outbound, 'expert', split_axis=0, concat_axis=0, tiled=True)  5.39 us
    all_to_all x1, starting transfers between devices, shards(): lax.all_to_all(my_cols.astype(jnp.bfloat16), 'expert', split_axis=0, conc...  4.59 us
  transfers between devices with their start and end apart: 3, of which 3 were waited for; matrix products, arithmetic and copies ran while one was open for 1% of the time, Pallas kernels for 0%

commit v1 on v0

--- a/solution.py
+++ b/solution.py
@@ -74,7 +74,11 @@
         .reshape(batch_rows, local_heads * head_dim)
     )
     partial_value = jnp.dot(attended, out_proj, preferred_element_type=jnp.float32)
-    attention = lax.psum(partial_value, "group")
+    attention = partial_value
+    for hop_ in (1, 2):
+        attention = attention + lax.ppermute(
+            attention, "group", [(dev, dev ^ hop_) for dev in range(4)]
+        )
     hidden = residual.astype(jnp.float32) + attention
     full_rows = lax.all_gather(hidden, "seq", axis=1, tiled=True)
     meansq = jnp.mean(full_rows * full_rows, axis=-1, keepdims=True)

time: 166 us -> 159 us (0.958)
  blocking collectives: 28.9 us -> 18.7 us
  waiting for transfers between devices: 62.5 us -> 64.6 us
  starting transfers between devices: 9.99 us -> 11.9 us
    psum x1 -> x0, blocking collectives: 10.3 us -> none  [shards(): attention = lax.psum(partial_value, 'group')]
    ppermute x0 -> x2, starting transfers between devices: none -> 2.08 us  [shards(): lax.ppermute(attention, 'group', [(dev, dev ^ hop_) for dev in range(4)])]
  transfers between devices with their start and end apart: 3 -> 5, of which waited for: 3 -> 4; matrix products, arithmetic and copies ran while one was open for 1% -> 3% of each run, Pallas kernels for 0% -> 0%
where the time goes in v1:
time: 159 us
  waiting for transfers between devices  64.6 us (41%)
  matrix products  40.5 us (25%)
  blocking collectives  18.7 us (12%)
  between operations  13.5 us (8%)
  starting transfers between devices  11.9 us (7%)
  other arithmetic  7.79 us (5%)
  local copies, waits for them, and re-layouts  1.72 us (1%)
    psum x1, waiting for transfers between devices, shards(): lax.psum(down_terms.astype(jnp.bfloat16), ('group', 'seq'))  52.6 us
    dot_general x1, matrix products, shards(): jnp.einsum('secf,efd->secd', activated, w_down, preferred_element_type=jn...  21.8 us
    all_gather x3, blocking collectives, combined_all(): everything = jax.tree.map(lambda part: lax.all_gather(part, axis), value)  14.1 us
    dot_general x1, matrix products, shards(): jnp.einsum('secd,edf->secf', inbound, w_gate, preferred_element_type=jnp....  11.6 us
    all_to_all x1, waiting for transfers between devices, shards(): lax.all_to_all(my_cols.astype(jnp.bfloat16), 'expert', split_axis=0, conc...  5.66 us
    all_to_all x1, starting transfers between devices, shards(): lax.all_to_all(outbound, 'expert', split_axis=0, concat_axis=0, tiled=True)  5.23 us
    all_to_all x1, waiting for transfers between devices, shards(): lax.all_to_all(outbound, 'expert', split_axis=0, concat_axis=0, tiled=True)  5.03 us
    all_to_all x1, starting transfers between devices, shards(): lax.all_to_all(my_cols.astype(jnp.bfloat16), 'expert', split_axis=0, conc...  4.59 us
  transfers between devices with their start and end apart: 5, of which 4 were waited for; matrix products, arithmetic and copies ran while one was open for 3% of the time, Pallas kernels for 0%

profile of v1, /device:TPU:0, one launch (start us, length us, event | category | flops | bytes accessed | tf_op | source)
XLA Modules:
  0.0 158.6 jit_solution(14023852185957612089)
XLA Ops:
  8.2 1.0 fusion.64
  9.3 5.3 %all-gather.1 = f32[8,2,4]{2,1,0:T(2,128)S(1)} all-gather(f32[4,2,4]{2,1,0:T(2,128)S(1)} %get-tuple-element.22), channel_id=3, replica_groups=mesh['group'=4,'seq'=2,'expert'=4] {'seq'}, dimensions={0}, use_global_device_ids=true | all-gather | bytes 384 | tf_op jit(solution)/shard_map/all_gather | solution.py:12
  14.7 1.2 fusion.29
  15.9 4.4 %all-gather = f32[8,2,4,128]{3,2,1,0:T(4,128)S(1)} all-gather(f32[4,2,4,128]{3,2,1,0:T(4,128)S(1)} %fusion.29), channel_id=2, replica_groups=mesh['group'=4,'seq'=2,'expert'=4] {'seq'}, dimensions={0}, use_global_device_ids=true | all-gather | bytes 49152 | tf_op jit(solution)/shard_map/all_gather | solution.py:12
  20.3 4.3 %all-gather.2 = f32[8,2,4]{2,1,0:T(2,128)S(1)} all-gather(f32[4,2,4]{2,1,0:T(2,128)S(1)} %fusion.44), channel_id=4, replica_groups=mesh['group'=4,'seq'=2,'expert'=4] {'seq'}, dimensions={0}, use_global_device_ids=true | all-gather | bytes 384 | tf_op jit(solution)/shard_map/all_gather | solution.py:12
  24.8 2.8 %fusion.65 = f32[4,2048]{1,0:T(4,128)S(1)} fusion(bf16[4,1024]{1,0:T(4,128)(2,1)S(1)} %reshape.183, bf16[1024,2048]{1,0:T(8,128)(2,1)} %param.18), kind=kOutput, calls=%fused_computation.72 | convolution fusion | flops 16777216 | bytes 4235264 | tf_op jit(solution)/shard_map/dot_general | solution.py:76
  27.7 0.8 fusion.56
  28.4 0.7 fusion.55
  29.2 0.9 select_reduce_fusion
  30.1 2.1 %collective-permute-start.1 = (f32[4,2048]{1,0:T(4,128)S(1)}, f32[4,2048]{1,0:T(4,128)S(1)}, u32[]{:S(2)}, u32[]{:S(2)}) collective-permute-start(f32[4,2048]{1,0:T(4,128)S(1)} %add.82), channel_id=1, source_target_pairs={{0,16},{8,24},{16,0},{24,8},{1,17},{9,25},{17,1},{25,9},{2,18},{10... | collective-permute-start | bytes 98312 | tf_op jit(solution)/shard_map/ppermute | solution.py:79
  33.0 1.3 collective-permute-done.1
  35.0 4.6 %all_gather.27 = f32[4,4096]{1,0:T(4,128)S(1)} all-gather(f32[4,2048]{1,0:T(4,128)S(1)} %add_add_fusion), channel_id=1, replica_groups=mesh['group'=4,'seq'=2,'expert'=4] {'seq'}, dimensions={1}, use_global_device_ids=true | all-gather | bytes 98304 | tf_op jit(solution)/shard_map/all_gather | solution.py:83
  39.9 1.0 fusion.66
  41.1 0.8 copy.42
  41.9 5.2 %all-to-all-start = ((bf16[4,2,2,4096]{3,2,1,0:T(2,128)(2,1)}), bf16[4,2,2,4096]{3,2,1,0:T(2,128)(2,1)S(1)}, u32[]{:S(2)}, u32[]{:S(2)}) async-start(bf16[4,2,2,4096]{3,2,1,0:T(2,128)(2,1)} %bitcast.2), calls=%async_computation | async-start | bytes 262144 | tf_op jit(solution)/shard_map/all_to_all | solution.py:110
  47.1 0.8 multiply_reduce_fusion.2
  48.0 5.0 %all-to-all-done = bf16[4,2,2,4096]{3,2,1,0:T(2,128)(2,1)S(1)} async-done(((bf16[4,2,2,4096]{3,2,1,0:T(2,128)(2,1)}), bf16[4,2,2,4096]{3,2,1,0:T(2,128)(2,1)S(1)}, u32[]{:S(2)}, u32[]{:S(2)}) %all-to-all-start) | async-done | bytes 131104 | tf_op jit(solution)/shard_map/all_to_all | solution.py:110
  53.0 11.6 %fusion.12 = f32[4,2,2,1792]{3,0,2,1:T(4,128)S(1)} fusion(bf16[2,4096,1792]{2,1,0:T(8,128)(2,1)} %param.23, bf16[4,2,2,4096]{3,2,1,0:T(2,128)(2,1)S(1)} %all-to-all-done), kind=kOutput, calls=%fused_computation.9 | convolution fusion | flops 234881024 | bytes 29605888 | tf_op jit(solution)/shard_map/secd,edf->secf/dot_general | solution.py:111
  64.6 21.8 %fusion.9 = bf16[4,2,2,4096]{3,0,2,1:T(4,128)(2,1)} fusion(bf16[2,1792,4096]{2,1,0:T(8,128)(2,1)} %param.25, bf16[2,4096,1792]{2,1,0:T(8,128)(2,1)} %param.24, f32[4,2,2,1792]{3,0,2,1:T(4,128)S(1)} %fusion.12, bf16[4,2,2,4096]{3,2,1,0:T(2,128)(2,1)S(1)} %all-to-all-done), kind=kOutput, calls=%fused_computation.8 | convolution fusion | flops 469999616 | bytes 59097088 | tf_op jit(solution)/shard_map/secf,efd->secd/dot_general | solution.py:114
  86.4 52.6 %all-reduce.2.cloned.1.call-done = bf16[4,2,2,4096]{3,0,2,1:T(4,128)(2,1)} async-done(((bf16[4,2,2,4096]{3,0,2,1:T(4,128)(2,1)}), bf16[4,2,2,4096]{3,0,2,1:T(4,128)(2,1)}) %all-reduce.2.cloned.1.call-update) | async-done | bytes 131088 | tf_op jit(solution)/shard_map/psum | solution.py:115
  139.1 0.9 convert_convert_fusion
  140.6 4.6 %all-to-all-start.1 = ((bf16[4,2,2,2048]{3,2,1,0:T(2,128)(2,1)}), bf16[4,2,2,2048]{3,2,1,0:T(2,128)(2,1)S(1)}, u32[]{:S(2)}, u32[]{:S(2)}) async-start(bf16[4,2,2,2048]{3,2,1,0:T(2,128)(2,1)} %copy.37), calls=%async_computation.1 | async-start | bytes 131072 | tf_op jit(solution)/shard_map/all_to_all | solution.py:118
  145.3 5.7 %all-to-all-done.1 = bf16[4,2,2,2048]{3,2,1,0:T(2,128)(2,1)S(1)} async-done(((bf16[4,2,2,2048]{3,2,1,0:T(2,128)(2,1)}), bf16[4,2,2,2048]{3,2,1,0:T(2,128)(2,1)S(1)}, u32[]{:S(2)}, u32[]{:S(2)}) %all-to-all-start.1) | async-done | bytes 65568 | tf_op jit(solution)/shard_map/all_to_all | solution.py:118
  151.0 0.8 fusion.27
  (32 shorter events, 4.9 us)
Async XLA Ops:
  6.5 1.7 %copy-start = (bf16[4,128,2,128]{3,2,1,0:T(2,128)(2,1)S(1)}, bf16[4,128,2,128]{3,2,1,0:T(2,128)(2,1)}, u32[]{:S(2)}) copy-start(bf16[4,128,2,128]{3,2,1,0:T(2,128)(2,1)} %param.14) | copy-start | bytes 786436
  27.7 2.5 %collective-permute-start = (f32[4,2048]{1,0:T(4,128)S(1)}, f32[4,2048]{1,0:T(4,128)S(1)}, u32[]{:S(2)}, u32[]{:S(2)}) collective-permute-start(f32[4,2048]{1,0:T(4,128)S(1)} %fusion.65), channel_id=1, source_target_pairs={{0,8},{8,0},{16,24},{24,16},{1,9},{9,1},{17,25},{25,17},{2,10},{10... | collective-permute-start | bytes 98312 | tf_op jit(solution)/shard_map/ppermute | solution.py:79
  30.1 4.1 %collective-permute-start.1 = (f32[4,2048]{1,0:T(4,128)S(1)}, f32[4,2048]{1,0:T(4,128)S(1)}, u32[]{:S(2)}, u32[]{:S(2)}) collective-permute-start(f32[4,2048]{1,0:T(4,128)S(1)} %add.82), channel_id=1, source_target_pairs={{0,16},{8,24},{16,0},{24,8},{1,17},{9,25},{17,1},{25,9},{2,18},{10... | collective-permute-start | bytes 98312 | tf_op jit(solution)/shard_map/ppermute | solution.py:79
  41.9 11.2 %all-to-all-start = ((bf16[4,2,2,4096]{3,2,1,0:T(2,128)(2,1)}), bf16[4,2,2,4096]{3,2,1,0:T(2,128)(2,1)S(1)}, u32[]{:S(2)}, u32[]{:S(2)}) async-start(bf16[4,2,2,4096]{3,2,1,0:T(2,128)(2,1)} %bitcast.2), calls=%async_computation | async-start | bytes 262144 | tf_op jit(solution)/shard_map/all_to_all | solution.py:110
  47.1 92.0 %all-reduce.2.cloned.1.call-start = ((), (), s32[]{:S(2)}) async-start(), calls=%async_computation.2 | async-start | bytes 262144 | tf_op jit(solution)/shard_map/psum | solution.py:115
  140.6 10.3 %all-to-all-start.1 = ((bf16[4,2,2,2048]{3,2,1,0:T(2,128)(2,1)}), bf16[4,2,2,2048]{3,2,1,0:T(2,128)(2,1)S(1)}, u32[]{:S(2)}, u32[]{:S(2)}) async-start(bf16[4,2,2,2048]{3,2,1,0:T(2,128)(2,1)} %copy.37), calls=%async_computation.1 | async-start | bytes 131072 | tf_op jit(solution)/shard_map/all_to_all | solution.py:118
Sparse Core Ops, SparseCore 0:
  86.6 52.4 all-reduce.1
